TPU v7x, 256 devices: a whole 4x4x8 slice. The times are simulated.
256 devices in a mesh: dp: 8 (over x, core), rows: 32 (over y, z).
Axes of the slice: x: 4, y: 4, z: 8, core: 2. Of those that a mesh axis runs over, the one named last changes fastest.
Arguments:
- grads: bfloat16 [2, 4096, 14336], P(None, 'rows', 'dp'), may hold values from -64 to 64
- basis: bfloat16 [2, 4096, 512], P(None, 'rows'), may hold values from -0.09375 to 0.09375
- moment1: float32 [2, 512, 14336], P(None, 'rows', 'dp'), may hold values from -0.3 to 0.3
- moment2: float32 [2, 512, 14336], P(None, 'rows', 'dp'), may hold values from 0.001 to 0.03
- weights: bfloat16 [2, 4096, 14336], P(None, 'rows', 'dp'), may hold values from -0.09375 to 0.09375
Outputs:
- new_weights: bfloat16 [2, 4096, 14336], P(None, 'rows')
- new_moment1: float32 [2, 512, 14336], P(None, 'rows', 'dp')
- new_moment2: float32 [2, 512, 14336], P(None, 'rows', 'dp')
All inputs are finite; a program needn't handle non-finite values.
Results may differ from a plain program's by a relative error of at most 0.00115.
The roundings to bfloat16 on the way count: a program that leaves them out, or rounds other values in their place, can miss the bound.
Values may be sent and summed in bfloat16 or wider, within the bound.
No kernel may reach another device: no remote copies, remote signals or barrier semaphores. Data moves between devices by JAX's collectives and lax.ppermute only.
A program may use at most 64 MiB of HBM per device.

v0:
```python
import math
import jax
import jax.numpy as jnp
from jax import lax
from jax.sharding import Mesh
from jax.sharding import PartitionSpec as P

D = 4096
FF = 14336
MATS = 2
STEP = 10
ROWS = ("rows_0", "rows_1")


def sum_by_axis(x, axes, dim):
    for axis in axes:
        x = lax.psum_scatter(x, axis, scatter_dimension=dim, tiled=True)
    return x


def laid_out(tiles, dim):
    tiles = jnp.moveaxis(tiles, 0, dim)
    shape = tiles.shape
    return tiles.reshape(*shape[:dim], shape[dim] * shape[dim + 1], *shape[dim + 2 :])


def gather_in_order(x, axes, turns):
    tiles = x[None]
    for k in turns:
        tiles = lax.all_gather(tiles, axes[k], axis=0, tiled=True)
    carried = [lax.axis_size(axes[k]) for k in reversed(turns)]
    tiles = tiles.reshape(*carried, *x.shape)
    turned = sorted(range(len(turns)), key=lambda place: turns[len(turns) - 1 - place])
    return tiles.transpose(*turned, *range(len(turns), tiles.ndim)).reshape(-1, *x.shape)


def whole_of(x, axes, turns, dim):
    return laid_out(gather_in_order(x, axes, turns), dim)


def moment_step(projected, moment1, moment2, total):
    limit = 1.0 * math.sqrt(MATS * D * FF)
    scale = limit / jnp.maximum(jnp.sqrt(total), limit)
    scaled = scale * projected
    first = 0.9 * moment1 + 0.1 * scaled
    second = 0.999 * moment2 + 0.001 * scaled * scaled
    first_bias_correction = 1.0 - 0.9**STEP
    second_fix = 1.0 - 0.999**STEP
    low_rank_update = (
        first / first_bias_correction / (jnp.sqrt(second / second_fix) + 1e-08)
    ).astype(jnp.bfloat16)
    return (first, second, low_rank_update)


def local(grads, basis, moment1, moment2, weights):
    grad_wide = grads.astype(jnp.float32)
    own_squares = jnp.sum(grad_wide * grad_wide)
    partial_norm_value = jnp.einsum(
        "yka,ykx->yax", basis, grads, preferred_element_type=jnp.float32
    )
    column_square_sum = jnp.full((lax.axis_size(ROWS),), own_squares, jnp.float32)
    projected, group_squares = (
        sum_by_axis(partial_norm_value, ROWS, 1),
        sum_by_axis(column_square_sum, ROWS, 0),
    )
    total = lax.psum(group_squares[0], "dp")
    first, second, low_rank_update = moment_step(projected, moment1, moment2, total)
    projected_back = jnp.einsum(
        "auw,awl->aul",
        basis,
        whole_of(low_rank_update, ROWS, (0, 1), 1),
        preferred_element_type=jnp.float32,
    )
    fresh = (weights.astype(jnp.float32) - 0.5 * projected_back).astype(jnp.bfloat16)
    whole_rows = lax.all_gather(fresh, "dp", axis=2, tiled=True)
    return (whole_rows, first, second)


def solution(mesh):
    finer = Mesh(mesh.devices.reshape(mesh.shape["dp"], 4, 8), ("dp", "rows_0", "rows_1"))
    in_specs = (
        P(None, ROWS, "dp"),
        P(None, ROWS, None),
        P(None, ROWS, "dp"),
        P(None, ROWS, "dp"),
        P(None, ROWS, "dp"),
    )
    out_specs = (P(None, ROWS, None), P(None, ROWS, "dp"), P(None, ROWS, "dp"))
    return jax.shard_map(local, mesh=finer, in_specs=in_specs, out_specs=out_specs, check_vma=False)
```

profile of v0, /device:TPU:1, one launch (start us, length us, event | category | flops | bytes accessed | tf_op | source)
XLA Modules:
  0.0 268.7 jit_solution(6423044746754964495)
XLA Ops:
  7.2 0.0 copy-start
  7.2 0.0 reduce-scatter.3.cloned.1.call-start
  7.2 0.9 copy-done
  8.1 5.4 %fusion.5 = f32[2,512,1792]{2,1,0:T(8,128)} fusion(bf16[2,128,512]{2,1,0:T(8,128)(2,1)S(1)} %copy-done, bf16[2,128,1792]{2,1,0:T(8,128)(2,1)} %param.5), kind=kOutput, calls=%fused_computation.9 | convolution fusion | flops 469762048 | bytes 8519680 | tf_op jit(solution)/shard_map/yka,ykx->yax/dot_general | solution.py:58
  13.5 0.0 copy-start.6
  13.5 0.0 copy-start.1
  13.5 0.0 copy-start.5
  13.5 0.0 copy-start.3
  13.5 0.0 copy-start.4
  13.5 0.0 reduce-scatter.3.cloned.1.call-update
  13.6 0.0 copy-start.2
  13.6 0.0 reduce-scatter.5.cloned.1.call-start
  13.6 78.9 %reduce-scatter.3.cloned.1.call-done = f32[2,128,1792]{2,1,0:T(8,128)} async-done(((f32[2,512,1792]{2,1,0:T(8,128)}), f32[2,128,1792]{2,1,0:T(8,128)}) %reduce-scatter.3.cloned.1.call-update) | async-done | bytes 1835024 | tf_op jit(solution)/shard_map/reduce_scatter | solution.py:17
  92.6 0.0 reduce-scatter.5.cloned.1.call-update
  92.6 0.0 all-gather.4.cloned.1.call-start
  92.6 0.0 copy-done.6
  92.6 0.6 dynamic-slice
  93.9 0.0 copy-done.1
  93.9 1.1 multiply_reduce_fusion
  95.0 0.6 broadcast_in_dim.6
  95.6 6.6 %all-reduce = f32[32]{0:T(128)S(1)} all-reduce(f32[32]{0:T(128)S(1)} %broadcast_in_dim.6), channel_id=3, replica_groups=mesh['dp'=8,'rows_0'=4,'rows_1'=8] {'rows_0'}, use_global_device_ids=true, to_apply=%region_1.0.clone | all-reduce | flops 32 | bytes 256
  102.2 0.1 dynamic-slice.1
  102.2 14.4 %all-reduce.1 = f32[8]{0:T(128)S(1)} all-reduce(f32[8]{0:T(128)S(1)} %dynamic-slice.1), channel_id=4, replica_groups=mesh['dp'=8,'rows_0'=4,'rows_1'=8] {'rows_1'}, use_global_device_ids=true, to_apply=%region_2.0.clone | all-reduce | flops 8 | bytes 64
  116.6 0.0 copy-done.5
  116.6 0.6 dynamic-slice.2
  117.2 1.2 dynamic-slice.3
  118.5 18.6 %psum.7 = f32[]{:T(128)} all-reduce(f32[]{:T(128)} %bitcast), channel_id=1, replica_groups=mesh['dp'=8,'rows_0'=4,'rows_1'=8] {'dp'}, use_global_device_ids=true, to_apply=%region_3.0 | all-reduce | flops 1 | bytes 8 | tf_op jit(solution)/shard_map/psum | solution.py:66
  137.8 0.0 reduce-scatter.5.cloned.1.call-done
  137.9 0.0 copy-done.3
  137.9 0.0 copy-done.4
  137.9 1.8 divide_convert_fusion
  139.7 10.5 %all-gather = bf16[8,16,1792]{2,1,0:T(8,128)(2,1)} all-gather(bf16[2,16,1792]{2,1,0:T(8,128)(2,1)S(1)} %get-tuple-element.12), channel_id=2, replica_groups=mesh['dp'=8,'rows_0'=4,'rows_1'=8] {'rows_0'}, dimensions={0}, use_global_device_ids=true | all-gather | bytes 573440 | tf_op jit(solution)/shard_map/all_gather | solution.py:30
  150.2 0.0 all-gather.4.cloned.1.call-update
  150.2 0.0 all-gather.6.cloned.1.call-start
  150.3 0.0 copy-done.2
  150.3 0.6 copy.17
  150.9 49.1 %all-gather.4.cloned.1.call-done = bf16[32,2,16,1792]{3,2,1,0:T(8,128)(2,1)} async-done(((bf16[4,2,16,1792]{3,2,1,0:T(8,128)(2,1)}), bf16[32,2,16,1792]{3,2,1,0:T(8,128)(2,1)}) %all-gather.4.cloned.1.call-update) | async-done | bytes 3670032 | tf_op jit(solution)/shard_map/all_gather | solution.py:30
  200.0 2.3 copy.19
  202.4 2.5 fusion.2
  204.9 0.0 all-gather.6.cloned.1.call-update
  204.9 47.1 %all-gather.6.cloned.1.call-done = bf16[2,128,14336]{1,2,0:T(8,128)(2,1)} async-done(((bf16[2,128,1792]{1,2,0:T(8,128)(2,1)}), bf16[2,128,14336]{1,2,0:T(8,128)(2,1)}) %all-gather.6.cloned.1.call-update) | async-done | bytes 7340048 | tf_op jit(solution)/shard_map/all_gather | solution.py:75
  252.0 10.1 %copy.21 = bf16[2,128,14336]{2,1,0:T(8,128)(2,1)} copy(bf16[2,128,14336]{1,2,0:T(8,128)(2,1)} %all-gather.6.cloned.1.call-done) | data formatting | bytes 14680064
Async XLA Ops:
  7.2 1.0 copy-start
  7.2 85.4 %reduce-scatter.3.cloned.1.call-start = ((), (), s32[]{:S(2)}) async-start(), calls=%async_computation.2 | async-start | bytes 9175040 | tf_op jit(solution)/shard_map/reduce_scatter | solution.py:17
  13.5 79.1 %copy-start.6 = (u32[256]{0:T(256)S(1)}, u32[256]{0:T(256)}, u32[]{:S(2)}) copy-start(u32[256]{0:T(256)} %constant.26) | copy-start | bytes 3076
  13.5 80.4 %copy-start.1 = (bf16[2,128,1792]{2,1,0:T(8,128)(2,1)S(1)}, bf16[2,128,1792]{2,1,0:T(8,128)(2,1)}, u32[]{:S(2)}) copy-start(bf16[2,128,1792]{2,1,0:T(8,128)(2,1)} %param.5) | copy-start | bytes 2752516
  13.5 103.1 %copy-start.5 = (u32[256]{0:T(256)S(1)}, u32[256]{0:T(256)}, u32[]{:S(2)}) copy-start(u32[256]{0:T(256)} %constant.30) | copy-start | bytes 3076
  13.5 124.3 %copy-start.3 = (f32[2,16,1792]{2,1,0:T(8,128)S(1)}, f32[2,16,1792]{2,1,0:T(8,128)}, u32[]{:S(2)}) copy-start(f32[2,16,1792]{2,1,0:T(8,128)} %param.7) | copy-start | bytes 688132
  13.5 124.4 %copy-start.4 = (f32[2,16,1792]{2,1,0:T(8,128)S(1)}, f32[2,16,1792]{2,1,0:T(8,128)}, u32[]{:S(2)}) copy-start(f32[2,16,1792]{2,1,0:T(8,128)} %param.8) | copy-start | bytes 688132
  13.6 136.7 %copy-start.2 = (bf16[2,128,1792]{2,1,0:T(8,128)(2,1)S(1)}, bf16[2,128,1792]{2,1,0:T(8,128)(2,1)}, u32[]{:S(2)}) copy-start(bf16[2,128,1792]{2,1,0:T(8,128)(2,1)} %param.9) | copy-start | bytes 2752516
  13.6 124.3 %reduce-scatter.5.cloned.1.call-start = ((), (), s32[]{:S(2)}) async-start(), calls=%async_computation.3 | async-start | bytes 2064384 | tf_op jit(solution)/shard_map/reduce_scatter | solution.py:17
  92.6 107.5 %all-gather.4.cloned.1.call-start = ((), (), s32[]{:S(2)}) async-start(), calls=%async_computation.4 | async-start | bytes 4128768 | tf_op jit(solution)/shard_map/all_gather | solution.py:30
  150.2 101.8 %all-gather.6.cloned.1.call-start = ((), (), s32[]{:S(2)}) async-start(), calls=%async_computation.5 | async-start | bytes 8257536 | tf_op jit(solution)/shard_map/all_gather | solution.py:75
Sparse Core Ops, SparseCore 0:
  13.7 78.8 reduce-scatter.2
  95.1 37.1 reduce-scatter.4
  150.4 49.6 all-gather.3
  205.0 46.9 all-gather.5
where the time goes:
time: 269 us
  waiting for transfers between devices  175 us (65%)
  blocking collectives  50.1 us (19%)
  local copies, waits for them, and re-layouts  17.1 us (6%)
  between operations  15.3 us (6%)
  matrix products  7.89 us (3%)
  other arithmetic  2.92 us (1%)
    reduce_scatter x2, waiting for transfers between devices, sum_by_axis(): x = lax.psum_scatter(x, axis, scatter_dimension=dim, tiled=True)  79 us
    all_gather x1, waiting for transfers between devices, gather_in_order(): tiles = lax.all_gather(tiles, axes[k], axis=0, tiled=True)  49.1 us
    all_gather x1, waiting for transfers between devices, local(): whole_rows = lax.all_gather(fresh, 'dp', axis=2, tiled=True)  47.1 us
    unnamed x2, blocking collectives  20.9 us
    psum x1, blocking collectives, local(): total = lax.psum(group_squares[0], 'dp')  18.6 us
    unnamed x20, local copies, waits for them, and re-layouts  14.2 us
    all_gather x1, blocking collectives, gather_in_order(): tiles = lax.all_gather(tiles, axes[k], axis=0, tiled=True)  10.5 us
    dot_general x1, matrix products, local(): jnp.einsum('yka,ykx->yax', basis, grads, preferred_element_type=jnp.float32)  5.38 us
  transfers between devices with their start and end apart: 4, of which 3 were waited for; matrix products, arithmetic and copies ran while one was open for 2% of the time, Pallas kernels for 0%

commit v1 on v0

--- a/solution.py
+++ b/solution.py
@@ -10,6 +10,19 @@
 MATS = 2
 STEP = 10
 ROWS = ("rows_0", "rows_1")
+
+
+def gather_around(x, axis, dim):
+    ways = lax.axis_size(axis)
+    up = [(d, (d + 1) % ways) for d in range(ways)]
+    down = [(d, (d - 1) % ways) for d in range(ways)]
+    earlier, later = ([x], [x])
+    for _ in range(ways // 2):
+        earlier.append(lax.ppermute(earlier[-1], axis, up))
+    for _ in range((ways - 1) // 2):
+        later.append(lax.ppermute(later[-1], axis, down))
+    line = jnp.concatenate([*earlier[::-1], *later[1:]], axis=dim)
+    return jnp.roll(line, (lax.axis_index(axis) - ways // 2) * x.shape[dim], axis=dim)
 
 
 def sum_by_axis(x, axes, dim):
@@ -72,7 +85,7 @@
         preferred_element_type=jnp.float32,
     )
     fresh = (weights.astype(jnp.float32) - 0.5 * projected_back).astype(jnp.bfloat16)
-    whole_rows = lax.all_gather(fresh, "dp", axis=2, tiled=True)
+    whole_rows = gather_around(fresh, "dp", 2)
     return (whole_rows, first, second)
 
 

time: 269 us -> 292 us (1.086); the launches traced: 269 us -> 286 us
  local copies, waits for them, and re-layouts: 17.1 us -> 31.5 us
  starting transfers between devices: 0.16 us -> 13.7 us
  waiting for transfers between devices: 175 us -> 166 us
    all_gather x1 -> x0, waiting for transfers between devices: 47.1 us -> none  [local(): whole_rows = lax.all_gather(fresh, 'dp', axis=2, tiled=True)]
    ppermute x0 -> x7, waiting for transfers between devices: none -> 37.6 us  [the longest x4 36.7 us: gather_around(): earlier.append(lax.ppermute(earlier[-1], axis, up))]
    ppermute x0 -> x7, starting transfers between devices: none -> 13.6 us  [the longest x4 9.47 us: gather_around(): earlier.append(lax.ppermute(earlier[-1], axis, up))]
    unnamed x20 -> x39, local copies, waits for them, and re-layouts: 14.2 us -> 24.4 us
    dynamic_slice x0 -> x1, local copies, waits for them, and re-layouts: none -> 4.04 us  [gather_around(): jnp.roll(line, (lax.axis_index(axis) - ways // 2) * x.shape[dim], axis=dim)]
  transfers between devices with their start and end apart: 4 -> 10, of which waited for: 3 -> 8; matrix products, arithmetic and copies ran while one was open for 2% -> 4% of each run, Pallas kernels for 0% -> 0%
where the time goes in v1:
time: 292 us; the launch traced here: 286 us
  waiting for transfers between devices  166 us (57%)
  blocking collectives  50.1 us (17%)
  local copies, waits for them, and re-layouts  31.5 us (11%)
  between operations  15.4 us (5%)
  starting transfers between devices  13.7 us (5%)
  matrix products  6.96 us (2%)
  other arithmetic  2.92 us (1%)
    reduce_scatter x2, waiting for transfers between devices, sum_by_axis(): x = lax.psum_scatter(x, axis, scatter_dimension=dim, tiled=True)  79 us
    all_gather x1, waiting for transfers between devices, gather_in_order(): tiles = lax.all_gather(tiles, axes[k], axis=0, tiled=True)  49.2 us
    ppermute x4, waiting for transfers between devices, gather_around(): earlier.append(lax.ppermute(earlier[-1], axis, up))  36.7 us
    unnamed x39, local copies, waits for them, and re-layouts  24.4 us
    unnamed x2, blocking collectives  20.9 us
    psum x1, blocking collectives, local(): total = lax.psum(group_squares[0], 'dp')  18.6 us
    all_gather x1, blocking collectives, gather_in_order(): tiles = lax.all_gather(tiles, axes[k], axis=0, tiled=True)  10.5 us
    ppermute x4, starting transfers between devices, gather_around(): earlier.append(lax.ppermute(earlier[-1], axis, up))  9.47 us
  transfers between devices with their start and end apart: 10, of which 8 were waited for; matrix products, arithmetic and copies ran while one was open for 4% of the time, Pallas kernels for 0%

profile of v1, /device:TPU:1, one launch (start us, length us, event | category | flops | bytes accessed | tf_op | source)
XLA Modules:
  0.0 286.3 jit_solution(5185082146796221445)
XLA Ops:
  7.2 0.0 copy-start
  7.2 0.0 copy-start.8
  7.2 0.0 copy-start.7
  7.2 0.0 reduce-scatter.3.cloned.1.call-start
  7.3 1.1 copy-done
  8.4 5.4 %fusion.5 = f32[2,512,1792]{2,1,0:T(8,128)} fusion(bf16[2,128,512]{2,1,0:T(8,128)(2,1)S(1)} %copy-done, bf16[2,128,1792]{2,1,0:T(8,128)(2,1)} %param.5), kind=kOutput, calls=%fused_computation.26 | convolution fusion | flops 469762048 | bytes 8519680 | tf_op jit(solution)/shard_map/yka,ykx->yax/dot_general | solution.py:71
  13.8 0.0 reduce-scatter.3.cloned.1.call-update
  13.8 0.0 reduce-scatter.5.cloned.1.call-start
  13.9 79.0 %reduce-scatter.3.cloned.1.call-done = f32[2,128,1792]{2,1,0:T(8,128)} async-done(((f32[2,512,1792]{2,1,0:T(8,128)}), f32[2,128,1792]{2,1,0:T(8,128)}) %reduce-scatter.3.cloned.1.call-update) | async-done | bytes 1835024 | tf_op jit(solution)/shard_map/reduce_scatter | solution.py:30
  92.8 0.0 reduce-scatter.5.cloned.1.call-update
  92.8 0.0 all-gather.3.cloned.1.call-start
  92.9 0.0 copy-done.8
  92.9 0.6 dynamic-slice
  94.1 0.0 copy-done.1
  94.1 1.1 multiply_reduce_fusion
  95.2 0.6 broadcast_in_dim.6
  95.9 6.6 %all-reduce = f32[32]{0:T(128)S(1)} all-reduce(f32[32]{0:T(128)S(1)} %broadcast_in_dim.6), channel_id=3, replica_groups=mesh['dp'=8,'rows_0'=4,'rows_1'=8] {'rows_0'}, use_global_device_ids=true, to_apply=%region_1.0.clone | all-reduce | flops 32 | bytes 256
  102.4 0.1 dynamic-slice.1
  102.5 14.4 %all-reduce.1 = f32[8]{0:T(128)S(1)} all-reduce(f32[8]{0:T(128)S(1)} %dynamic-slice.1), channel_id=4, replica_groups=mesh['dp'=8,'rows_0'=4,'rows_1'=8] {'rows_1'}, use_global_device_ids=true, to_apply=%region_2.0.clone | all-reduce | flops 8 | bytes 64
  116.9 0.6 dynamic-slice.2
  117.5 1.2 dynamic-slice.3
  118.7 18.6 %psum.7 = f32[]{:T(128)} all-reduce(f32[]{:T(128)} %bitcast), channel_id=1, replica_groups=mesh['dp'=8,'rows_0'=4,'rows_1'=8] {'dp'}, use_global_device_ids=true, to_apply=%region_3.0 | all-reduce | flops 1 | bytes 8 | tf_op jit(solution)/shard_map/psum | solution.py:79
  138.1 0.0 reduce-scatter.5.cloned.1.call-done
  138.1 0.0 copy-done.5
  138.1 0.0 copy-done.6
  138.1 1.8 divide_convert_fusion
  140.0 10.5 %all-gather = bf16[8,16,1792]{2,1,0:T(8,128)(2,1)} all-gather(bf16[2,16,1792]{2,1,0:T(8,128)(2,1)S(1)} %get-tuple-element.12), channel_id=2, replica_groups=mesh['dp'=8,'rows_0'=4,'rows_1'=8] {'rows_0'}, dimensions={0}, use_global_device_ids=true | all-gather | bytes 573440 | tf_op jit(solution)/shard_map/all_gather | solution.py:43
  150.5 0.0 all-gather.3.cloned.1.call-update
  150.5 0.6 copy.17
  151.1 49.2 %all-gather.3.cloned.1.call-done = bf16[32,2,16,1792]{3,2,1,0:T(8,128)(2,1)} async-done(((bf16[4,2,16,1792]{3,2,1,0:T(8,128)(2,1)}), bf16[32,2,16,1792]{3,2,1,0:T(8,128)(2,1)}) %all-gather.3.cloned.1.call-update) | async-done | bytes 3670032 | tf_op jit(solution)/shard_map/all_gather | solution.py:43
  200.3 2.3 copy.19
  202.6 1.6 fusion.2
  204.2 1.9 collective-permute-start
  206.2 10.3 %collective-permute-done = bf16[2,128,1792]{1,2,0:T(8,128)(2,1)S(1)} collective-permute-done((bf16[2,128,1792]{1,2,0:T(8,128)(2,1)S(1)}, bf16[2,128,1792]{1,2,0:T(8,128)(2,1)S(1)}, u32[]{:S(2)}, u32[]{:S(2)}) %collective-permute-start) | collective-permute-done | bytes 917536 | tf_op jit(solution)/shard_map/ppermute | solution.py:21
  216.5 2.5 collective-permute-start.1
  219.0 0.1 collective-permute-start.4
  219.1 10.2 %collective-permute-done.1 = bf16[2,128,1792]{1,2,0:T(8,128)(2,1)S(1)} collective-permute-done((bf16[2,128,1792]{1,2,0:T(8,128)(2,1)S(1)}, bf16[2,128,1792]{1,2,0:T(8,128)(2,1)S(1)}, u32[]{:S(2)}, u32[]{:S(2)}) %collective-permute-start.1) | collective-permute-done | bytes 917536 | tf_op jit(solution)/shard_map/ppermute | solution.py:21
  229.3 2.5 collective-permute-start.2
  231.8 0.3 collective-permute-done.4
  232.1 2.0 collective-permute-start.5
  234.1 8.1 %collective-permute-done.2 = bf16[2,128,1792]{1,2,0:T(8,128)(2,1)} collective-permute-done((bf16[2,128,1792]{1,2,0:T(8,128)(2,1)S(1)}, bf16[2,128,1792]{1,2,0:T(8,128)(2,1)}, u32[]{:S(2)}, u32[]{:S(2)}) %collective-permute-start.2) | collective-permute-done | bytes 917536 | tf_op jit(solution)/shard_map/ppermute | solution.py:21
  242.1 2.6 collective-permute-start.3
  244.7 0.6 collective-permute-done.5
  245.3 2.0 collective-permute-start.6
  247.3 8.1 %collective-permute-done.3 = bf16[2,128,1792]{1,2,0:T(8,128)(2,1)} collective-permute-done((bf16[2,128,1792]{1,2,0:T(8,128)(2,1)}, bf16[2,128,1792]{1,2,0:T(8,128)(2,1)}, u32[]{:S(2)}, u32[]{:S(2)}) %collective-permute-start.3) | collective-permute-done | bytes 917536 | tf_op jit(solution)/shard_map/ppermute | solution.py:21
  255.4 1.2 constant_dynamic-update-slice_fusion.15
  256.6 1.3 constant_dynamic-update-slice_fusion.14
  257.9 1.3 constant_dynamic-update-slice_fusion.13
  259.2 0.1 constant_dynamic-update-slice_fusion.12
  259.4 0.1 constant_dynamic-update-slice_fusion.11
  259.5 0.1 constant_dynamic-update-slice_fusion.10
  259.6 1.3 constant_dynamic-update-slice_fusion.9
  260.9 0.0 collective-permute-done.6
  260.9 0.1 constant_dynamic-update-slice_fusion.8
  261.0 1.3 constant_dynamic-update-slice_fusion.7
  262.4 1.3 constant_dynamic-update-slice_fusion.6
  263.7 0.1 constant_dynamic-update-slice_fusion.5
  263.8 0.1 constant_dynamic-update-slice_fusion.4
  263.9 0.1 constant_dynamic-update-slice_fusion.3
  264.0 0.1 constant_dynamic-update-slice_fusion.2
  264.2 1.3 constant_dynamic-update-slice_fusion.1
  265.5 0.1 constant_dynamic-update-slice_fusion
  265.6 4.0 %constant_dynamic-slice_fusion = bf16[2,128,14336]{1,2,0:T(8,128)(2,1)} fusion(bf16[2,128,28672]{1,2,0:T(8,128)(2,1)S(1)} %constant_dynamic-update-slice_fusion, s32[]{:T(128)S(6)} %select_n.14), kind=kLoop, calls=%fused_computation.25 | loop fusion | bytes 14680068 | tf_op jit(solution)/shard_map/jit(_roll_dynamic)/dynamic_slice | solution.py:25
  269.7 10.1 %copy.21 = bf16[2,128,14336]{2,1,0:T(8,128)(2,1)} copy(bf16[2,128,14336]{1,2,0:T(8,128)(2,1)} %constant_dynamic-slice_fusion) | data formatting | bytes 14680064
  (10 shorter events, 0.0 us)
Async XLA Ops:
  7.2 1.2 copy-start
  7.2 85.7 %copy-start.8 = (u32[256]{0:T(256)S(1)}, u32[256]{0:T(256)}, u32[]{:S(2)}) copy-start(u32[256]{0:T(256)} %constant.56) | copy-start | bytes 3076
  7.2 109.7 %copy-start.7 = (u32[256]{0:T(256)S(1)}, u32[256]{0:T(256)}, u32[]{:S(2)}) copy-start(u32[256]{0:T(256)} %constant.60) | copy-start | bytes 3076
  7.2 86.9 %copy-start.1 = (bf16[2,128,1792]{2,1,0:T(8,128)(2,1)S(1)}, bf16[2,128,1792]{2,1,0:T(8,128)(2,1)}, u32[]{:S(2)}) copy-start(bf16[2,128,1792]{2,1,0:T(8,128)(2,1)} %param.5) | copy-start | bytes 2752516
  7.2 130.9 %copy-start.5 = (f32[2,16,1792]{2,1,0:T(8,128)S(1)}, f32[2,16,1792]{2,1,0:T(8,128)}, u32[]{:S(2)}) copy-start(f32[2,16,1792]{2,1,0:T(8,128)} %param.7) | copy-start | bytes 688132
  7.2 130.9 %copy-start.6 = (f32[2,16,1792]{2,1,0:T(8,128)S(1)}, f32[2,16,1792]{2,1,0:T(8,128)}, u32[]{:S(2)}) copy-start(f32[2,16,1792]{2,1,0:T(8,128)} %param.8) | copy-start | bytes 688132
  7.2 143.3 %copy-start.4 = (bf16[2,128,1792]{2,1,0:T(8,128)(2,1)S(1)}, bf16[2,128,1792]{2,1,0:T(8,128)(2,1)}, u32[]{:S(2)}) copy-start(bf16[2,128,1792]{2,1,0:T(8,128)(2,1)} %param.9) | copy-start | bytes 2752516
  7.2 85.6 %reduce-scatter.3.cloned.1.call-start = ((), (), s32[]{:S(2)}) async-start(), calls=%async_computation.2 | async-start | bytes 9175040 | tf_op jit(solution)/shard_map/reduce_scatter | solution.py:30
  13.8 124.3 %reduce-scatter.5.cloned.1.call-start = ((), (), s32[]{:S(2)}) async-start(), calls=%async_computation.3 | async-start | bytes 2064384 | tf_op jit(solution)/shard_map/reduce_scatter | solution.py:30
  92.8 107.5 %all-gather.3.cloned.1.call-start = ((), (), s32[]{:S(2)}) async-start(), calls=%async_computation.4 | async-start | bytes 4128768 | tf_op jit(solution)/shard_map/all_gather | solution.py:43
  204.2 12.3 %collective-permute-start = (bf16[2,128,1792]{1,2,0:T(8,128)(2,1)S(1)}, bf16[2,128,1792]{1,2,0:T(8,128)(2,1)S(1)}, u32[]{:S(2)}, u32[]{:S(2)}) collective-permute-start(bf16[2,128,1792]{1,2,0:T(8,128)(2,1)S(1)} %fusion.2), channel_id=1, source_target_pairs={{0,32},{32,64},{64,96},{96,128},{128,160},{160,192},{192,224},{224... | collective-permute-start | bytes 2752520 | tf_op jit(solution)/shard_map/ppermute | solution.py:21
  216.5 12.8 %collective-permute-start.1 = (bf16[2,128,1792]{1,2,0:T(8,128)(2,1)S(1)}, bf16[2,128,1792]{1,2,0:T(8,128)(2,1)S(1)}, u32[]{:S(2)}, u32[]{:S(2)}) collective-permute-start(bf16[2,128,1792]{1,2,0:T(8,128)(2,1)S(1)} %collective-permute-done), channel_id=1, source_target_pairs={{0,32},{32,64},{64,96},{96,128},{128,160},{160,192},{192,224},{224... | collective-permute-start | bytes 2752520 | tf_op jit(solution)/shard_map/ppermute | solution.py:21
  219.0 13.1 %collective-permute-start.4 = (bf16[2,128,1792]{1,2,0:T(8,128)(2,1)S(1)}, bf16[2,128,1792]{1,2,0:T(8,128)(2,1)S(1)}, u32[]{:S(2)}, u32[]{:S(2)}) collective-permute-start(bf16[2,128,1792]{1,2,0:T(8,128)(2,1)S(1)} %fusion.2), channel_id=1, source_target_pairs={{0,224},{32,0},{64,32},{96,64},{128,96},{160,128},{192,160},{224,1... | collective-permute-start | bytes 2752520 | tf_op jit(solution)/shard_map/ppermute | solution.py:23
  229.3 2.8 copy-start.2
  229.3 12.8 %collective-permute-start.2 = (bf16[2,128,1792]{1,2,0:T(8,128)(2,1)S(1)}, bf16[2,128,1792]{1,2,0:T(8,128)(2,1)}, u32[]{:S(2)}, u32[]{:S(2)}) collective-permute-start(bf16[2,128,1792]{1,2,0:T(8,128)(2,1)S(1)} %collective-permute-done.1), channel_id=1, source_target_pairs={{0,32},{32,64},{64,96},{96,128},{128,160},{160,192},{192,224},{224... | collective-permute-start | bytes 2752520 | tf_op jit(solution)/shard_map/ppermute | solution.py:21
  232.1 13.2 %collective-permute-start.5 = (bf16[2,128,1792]{1,2,0:T(8,128)(2,1)S(1)}, bf16[2,128,1792]{1,2,0:T(8,128)(2,1)}, u32[]{:S(2)}, u32[]{:S(2)}) collective-permute-start(bf16[2,128,1792]{1,2,0:T(8,128)(2,1)S(1)} %collective-permute-done.4), channel_id=1, source_target_pairs={{0,224},{32,0},{64,32},{96,64},{128,96},{160,128},{192,160},{224,1... | collective-permute-start | bytes 2752520 | tf_op jit(solution)/shard_map/ppermute | solution.py:23
  242.1 13.2 %collective-permute-start.3 = (bf16[2,128,1792]{1,2,0:T(8,128)(2,1)}, bf16[2,128,1792]{1,2,0:T(8,128)(2,1)}, u32[]{:S(2)}, u32[]{:S(2)}) collective-permute-start(bf16[2,128,1792]{1,2,0:T(8,128)(2,1)} %collective-permute-done.2), channel_id=1, source_target_pairs={{0,32},{32,64},{64,96},{96,128},{128,160},{160,192},{192,224},{224... | collective-permute-start | bytes 2752520 | tf_op jit(solution)/shard_map/ppermute | solution.py:21
  244.7 18.9 %copy-start.3 = (bf16[2,128,1792]{1,2,0:T(8,128)(2,1)S(1)}, bf16[2,128,1792]{1,2,0:T(8,128)(2,1)}, u32[]{:S(2)}) copy-start(bf16[2,128,1792]{1,2,0:T(8,128)(2,1)} %copy-done.2) | copy-start | bytes 2752516
  245.3 15.6 %collective-permute-start.6 = (bf16[2,128,1792]{1,2,0:T(8,128)(2,1)}, bf16[2,128,1792]{1,2,0:T(8,128)(2,1)S(1)}, u32[]{:S(2)}, u32[]{:S(2)}) collective-permute-start(bf16[2,128,1792]{1,2,0:T(8,128)(2,1)} %collective-permute-done.5), channel_id=1, source_target_pairs={{0,224},{32,0},{64,32},{96,64},{128,96},{160,128},{192,160},{224,1... | collective-permute-start | bytes 2752520 | tf_op jit(solution)/shard_map/ppermute | solution.py:23
Sparse Core Ops, SparseCore 0:
  13.9 78.8 reduce-scatter.2
  95.4 37.1 reduce-scatter.4
  150.6 49.6 all-gather.2
